TPU v7x, 32 devices: a whole 2x2x4 slice. The times are simulated.
32 devices in a mesh: groups: 2 (over y), rows: 4 (over z), cols: 2 (over x), sub: 2 (over core).
Axes of the slice: x: 2, y: 2, z: 4, core: 2. Of those that a mesh axis runs over, the one named last changes fastest.
Arguments:
- returns: float32 [8, 64, 8192], P('groups', 'rows', ('cols', 'sub')), parts along dimension 0, may hold values from -6 to 6
- starts: int32 [8, 8192], P('groups', ('cols', 'sub')), parts along dimension 0, may hold values from 0 to 32
- start_block: float32 [8, 32, 8192], P('groups', None, ('cols', 'sub')), parts along dimension 0, may hold values from -6 to 6
Outputs:
- loadings: float32 [8, 32, 8192], P('groups', None, ('cols', 'sub')), parts along dimension 0
There are 2 independent parts, one for each index of `groups`. A program takes and returns all parts, laid end to end along the dimension named above; each array names one. Nothing has to cross between parts.
Inputs may be any that keep to these rules, and one draw needn't show every extreme that they name: `starts`: days before an asset's start day hold returns that do not count.
All inputs are finite; a program needn't handle non-finite values.
Results may differ from a plain program's by a relative error of at most 0.0078.
Values may be sent and summed in bfloat16 or wider, within the bound.
A program may use at most 64 MiB of HBM per device.

v0:
```python
import jax
import jax.numpy as jnp
from jax import lax
from jax.sharding import PartitionSpec as P

ASSETS = 8192
ITERS = 3


def gram_of(image):
    return jnp.einsum("wkj,wlj->wkl", image, image, precision=lax.Precision.HIGHEST)


def project(factors, scaled):
    rounded = factors.astype(jnp.bfloat16)
    return jnp.einsum("wka,wta->wkt", rounded, scaled, preferred_element_type=jnp.float32)


def expand(proj, widened):
    return jnp.einsum("wkt,wta->wka", proj, widened, precision=lax.Precision.HIGHEST)


def orthonormal(image, gram):
    lower = jnp.linalg.cholesky(gram / ASSETS)
    return jax.scipy.linalg.solve_triangular(lower, image, lower=True)


def on_device(returns, starts, start_block):
    windows, days, width = returns.shape
    rows_count = lax.axis_size("rows")
    row_pos = lax.axis_index("rows")
    total_days = days * rows_count
    day_index = row_pos * days + jnp.arange(days, dtype=jnp.int32)
    live = (day_index[None, :, None] >= starts[:, None, :]).astype(jnp.float32)
    counts = (total_days - starts).astype(jnp.float32)
    masked = live * returns
    sums = lax.psum(jnp.sum(masked, axis=1), "rows")
    mean = sums / counts
    centered = live * (returns - mean[:, None, :])
    squares = lax.psum(jnp.sum(centered * centered, axis=1), "rows")
    scaled = (centered * lax.rsqrt(squares + 1.0)[:, None, :]).astype(jnp.bfloat16)
    widened = scaled.astype(jnp.float32)
    factors = start_block
    for step in range(ITERS):
        proj = lax.psum(project(factors, scaled), ("cols", "sub"))
        image = lax.psum(expand(proj, widened), "rows")
        gram = lax.psum(gram_of(image), ("cols", "sub"))
        factors = orthonormal(image, gram)
    return factors


def solution(mesh):
    placed = (
        P("groups", "rows", ("cols", "sub")),
        P("groups", ("cols", "sub")),
        P("groups", None, ("cols", "sub")),
    )
    return jax.shard_map(
        on_device,
        mesh=mesh,
        in_specs=placed,
        out_specs=P("groups", None, ("cols", "sub")),
        check_vma=False,
    )
```

profile of v0, /device:TPU:0, one launch (start us, length us, event | category | flops | bytes accessed | tf_op | source)
XLA Modules:
  0.0 354.8 jit_solution(6312155068273593770)
XLA Ops:
  6.5 0.0 all-reduce.4.cloned.1.call-start
  6.5 1.3 fusion
  7.8 0.0 copy-start.4
  7.9 20.9 %psum.77 = f32[4,2048]{1,0:T(4,128)S(1)} all-reduce(f32[4,2048]{1,0:T(4,128)S(1)} %fusion), channel_id=1, replica_groups=mesh['groups'=2,'rows'=4,'cols'=2,'sub'=2] {'rows'}, use_global_device_ids=true, to_apply=%region_1.0 | all-reduce | flops 8192 | bytes 65536 | tf_op jit(solution)/shard_map/psum | solution.py:37
  28.9 0.2 multiply_reduce_fusion
  29.1 15.8 %psum.78 = f32[4,2048]{1,0:T(4,128)S(1)} all-reduce(f32[4,2048]{1,0:T(4,128)S(1)} %multiply_reduce_fusion), channel_id=1, replica_groups=mesh['groups'=2,'rows'=4,'cols'=2,'sub'=2] {'rows'}, use_global_device_ids=true, to_apply=%region_3.0 | all-reduce | flops 8192 | bytes 65536 | tf_op jit(solution)/shard_map/psum | solution.py:40
  44.9 0.2 multiply_convert_fusion
  45.1 0.2 convolution_bitcast_fusion
  45.3 10.3 %psum.79 = f32[4,32,16]{1,2,0:T(8,128)S(1)} all-reduce(f32[4,32,16]{1,2,0:T(8,128)S(1)} %convolution_bitcast_fusion), channel_id=1, replica_groups=mesh['groups'=2,'rows'=4,'cols'=2,'sub'=2] {'cols','sub'}, use_global_device_ids=true, to_apply=%region_4.0 | all-reduce | flops 2048 | bytes 16384 | tf_op jit(solution)/shard_map/psum | solution.py:45
  55.6 1.6 fusion.9
  57.2 0.0 all-reduce.4.cloned.1.call-update
  57.2 0.0 all-reduce.6.cloned.1.call-start
  57.3 51.6 %all-reduce.4.cloned.1.call-done = f32[4,32,2048]{2,1,0:T(8,128)} async-done(((f32[4,32,2048]{2,1,0:T(8,128)}), f32[4,32,2048]{2,1,0:T(8,128)}) %all-reduce.4.cloned.1.call-update) | async-done | bytes 1048592 | tf_op jit(solution)/shard_map/psum | solution.py:46
  108.8 2.7 fusion.10
  111.6 11.8 %psum.81 = f32[4,32,32]{1,2,0:T(8,128)S(1)} all-reduce(f32[4,32,32]{1,2,0:T(8,128)S(1)} %fusion.10), channel_id=1, replica_groups=mesh['groups'=2,'rows'=4,'cols'=2,'sub'=2] {'cols','sub'}, use_global_device_ids=true, to_apply=%region_6.0 | all-reduce | flops 4096 | bytes 32768 | tf_op jit(solution)/shard_map/psum | solution.py:47
  123.4 0.1 copy.12
  123.6 11.7 %custom-call.10 = f32[4,32,32]{2,1,0:T(8,128)S(1)} custom-call(f32[4,32,32]{2,1,0:T(8,128)S(1)} %fusion.8), custom_call_target="Cholesky" | custom-call | tf_op jit(solution)/shard_map/jit(cholesky)/cholesky | solution.py:24
  135.3 0.1 compare_reduce_fusion.2
  135.4 0.1 select_bitcast_fusion.2
  135.5 9.8 %custom-call.11 = f32[4,1,32,32]{2,3,1,0:T(8,128)S(1)} custom-call(f32[4,1,32,32]{3,2,1,0:T(8,128)S(1)} %select_bitcast_fusion.2), custom_call_target="InvertDiagBlocksLowerTriangular" | custom-call | tf_op jit(solution)/shard_map/jit(_solve_triangular)/vmap()/triangular_solve | solution.py:25
  145.4 1.1 convolution_convert_fusion.1
  146.4 0.2 fusion.11
  146.7 10.5 %psum.82 = f32[4,32,16]{1,2,0:T(8,128)S(1)} all-reduce(f32[4,32,16]{1,2,0:T(8,128)S(1)} %fusion.11), channel_id=1, replica_groups=mesh['groups'=2,'rows'=4,'cols'=2,'sub'=2] {'cols','sub'}, use_global_device_ids=true, to_apply=%region_9.0 | all-reduce | flops 2048 | bytes 16384 | tf_op jit(solution)/shard_map/psum | solution.py:45
  157.2 1.6 fusion.12
  158.8 0.0 all-reduce.6.cloned.1.call-update
  158.8 0.0 all-reduce.8.cloned.1.call-start
  158.8 50.5 %all-reduce.6.cloned.1.call-done = f32[4,32,2048]{2,1,0:T(8,128)} async-done(((f32[4,32,2048]{2,1,0:T(8,128)}), f32[4,32,2048]{2,1,0:T(8,128)}) %all-reduce.6.cloned.1.call-update) | async-done | bytes 1048592 | tf_op jit(solution)/shard_map/psum | solution.py:46
  209.3 2.7 fusion.13
  212.0 11.8 %psum.84 = f32[4,32,32]{1,2,0:T(8,128)S(1)} all-reduce(f32[4,32,32]{1,2,0:T(8,128)S(1)} %fusion.13), channel_id=1, replica_groups=mesh['groups'=2,'rows'=4,'cols'=2,'sub'=2] {'cols','sub'}, use_global_device_ids=true, to_apply=%region_11.0 | all-reduce | flops 4096 | bytes 32768 | tf_op jit(solution)/shard_map/psum | solution.py:47
  223.9 0.1 copy.14
  224.0 11.7 %custom-call.12 = f32[4,32,32]{2,1,0:T(8,128)S(1)} custom-call(f32[4,32,32]{2,1,0:T(8,128)S(1)} %fusion.6), custom_call_target="Cholesky" | custom-call | tf_op jit(solution)/shard_map/jit(cholesky)/cholesky | solution.py:24
  235.8 0.1 compare_reduce_fusion.1
  235.9 0.1 select_bitcast_fusion.1
  236.0 9.8 %custom-call.13 = f32[4,1,32,32]{2,3,1,0:T(8,128)S(1)} custom-call(f32[4,1,32,32]{3,2,1,0:T(8,128)S(1)} %select_bitcast_fusion.1), custom_call_target="InvertDiagBlocksLowerTriangular" | custom-call | tf_op jit(solution)/shard_map/jit(_solve_triangular)/vmap()/triangular_solve | solution.py:25
  245.8 1.1 convolution_convert_fusion
  246.9 0.2 fusion.14
  247.1 10.5 %psum.85 = f32[4,32,16]{1,2,0:T(8,128)S(1)} all-reduce(f32[4,32,16]{1,2,0:T(8,128)S(1)} %fusion.14), channel_id=1, replica_groups=mesh['groups'=2,'rows'=4,'cols'=2,'sub'=2] {'cols','sub'}, use_global_device_ids=true, to_apply=%region_12.0 | all-reduce | flops 2048 | bytes 16384 | tf_op jit(solution)/shard_map/psum | solution.py:45
  257.6 1.6 fusion.15
  259.2 0.0 all-reduce.8.cloned.1.call-update
  259.2 50.5 %all-reduce.8.cloned.1.call-done = f32[4,32,2048]{2,1,0:T(8,128)} async-done(((f32[4,32,2048]{2,1,0:T(8,128)}), f32[4,32,2048]{2,1,0:T(8,128)}) %all-reduce.8.cloned.1.call-update) | async-done | bytes 1048592 | tf_op jit(solution)/shard_map/psum | solution.py:46
  309.7 2.7 fusion.16
  312.5 11.8 %psum.87 = f32[4,32,32]{1,2,0:T(8,128)S(1)} all-reduce(f32[4,32,32]{1,2,0:T(8,128)S(1)} %fusion.16), channel_id=1, replica_groups=mesh['groups'=2,'rows'=4,'cols'=2,'sub'=2] {'cols','sub'}, use_global_device_ids=true, to_apply=%region_14.17 | all-reduce | flops 4096 | bytes 32768 | tf_op jit(solution)/shard_map/psum | solution.py:47
  324.4 0.1 copy.16
  324.5 11.7 %custom-call.14 = f32[4,32,32]{2,1,0:T(8,128)S(1)} custom-call(f32[4,32,32]{2,1,0:T(8,128)S(1)} %fusion.4), custom_call_target="Cholesky" | custom-call | tf_op jit(solution)/shard_map/jit(cholesky)/cholesky | solution.py:24
  336.2 0.1 compare_reduce_fusion
  336.3 0.1 select_bitcast_fusion
  336.4 9.8 %custom-call.15 = f32[4,1,32,32]{2,3,1,0:T(8,128)S(1)} custom-call(f32[4,1,32,32]{3,2,1,0:T(8,128)S(1)} %select_bitcast_fusion), custom_call_target="InvertDiagBlocksLowerTriangular" | custom-call | tf_op jit(solution)/shard_map/jit(_solve_triangular)/vmap()/triangular_solve | solution.py:25
  346.3 2.0 fusion.2
  (25 shorter events, 0.2 us)
Async XLA Ops:
  6.5 22.3 %copy-start.3 = (f32[4,16,2048]{2,1,0:T(8,128)S(1)}, f32[4,16,2048]{2,1,0:T(8,128)}, u32[]{:S(2)}) copy-start(f32[4,16,2048]{2,1,0:T(8,128)} %param.6) | copy-start | bytes 1572868
  6.5 102.3 %all-reduce.4.cloned.1.call-start = ((), (), s32[]{:S(2)}) async-start(), calls=%async_computation | async-start | bytes 2097152 | tf_op jit(solution)/shard_map/psum | solution.py:46
  6.5 22.3 %copy-start.5 = (s32[4,2048]{1,0:T(4,128)S(1)}, s32[4,2048]{1,0:T(4,128)}, u32[]{:S(2)}) copy-start(s32[4,2048]{1,0:T(4,128)} %param.7) | copy-start | bytes 98308
  7.8 37.2 %copy-start.4 = (f32[4,32,2048]{2,1,0:T(8,128)S(1)}, f32[4,32,2048]{2,1,0:T(8,128)}, u32[]{:S(2)}) copy-start(f32[4,32,2048]{2,1,0:T(8,128)} %param.8) | copy-start | bytes 3145732
  57.2 152.1 %all-reduce.6.cloned.1.call-start = ((), (), s32[]{:S(2)}) async-start(), calls=%async_computation.1 | async-start | bytes 2097152 | tf_op jit(solution)/shard_map/psum | solution.py:46
  108.8 36.5 %copy-start = (f32[4,32,2048]{2,1,0:T(8,128)S(1)}, f32[4,32,2048]{2,1,0:T(8,128)}, u32[]{:S(2)}) copy-start(f32[4,32,2048]{2,1,0:T(8,128)} %all-reduce.4.cloned.1.call-done) | copy-start | bytes 3145732
  158.8 151.0 %all-reduce.8.cloned.1.call-start = ((), (), s32[]{:S(2)}) async-start(), calls=%async_computation.2 | async-start | bytes 2097152 | tf_op jit(solution)/shard_map/psum | solution.py:46
  209.3 36.5 %copy-start.1 = (f32[4,32,2048]{2,1,0:T(8,128)S(1)}, f32[4,32,2048]{2,1,0:T(8,128)}, u32[]{:S(2)}) copy-start(f32[4,32,2048]{2,1,0:T(8,128)} %all-reduce.6.cloned.1.call-done) | copy-start | bytes 3145732
  309.7 36.5 %copy-start.2 = (f32[4,32,2048]{2,1,0:T(8,128)S(1)}, f32[4,32,2048]{2,1,0:T(8,128)}, u32[]{:S(2)}) copy-start(f32[4,32,2048]{2,1,0:T(8,128)} %all-reduce.8.cloned.1.call-done) | copy-start | bytes 3145732
Sparse Core Ops, SparseCore 0:
  57.3 51.4 all-reduce.3
  158.9 50.3 all-reduce.5
  259.3 50.3 all-reduce.7
where the time goes:
time: 355 us
  waiting for transfers between devices  153 us (43%)
  blocking collectives  103 us (29%)
  other arithmetic  67.2 us (19%)
  matrix products  17.9 us (5%)
  between operations  13.4 us (4%)
    psum x3, waiting for transfers between devices, on_device(): image = lax.psum(expand(proj, widened), 'rows')  153 us
    another operation x10, other arithmetic, orthonormal(): lower = jnp.linalg.cholesky(gram / ASSETS)  35.6 us
    psum x3, blocking collectives, on_device(): gram = lax.psum(gram_of(image), ('cols', 'sub'))  35.5 us
    psum x3, blocking collectives, on_device(): proj = lax.psum(project(factors, scaled), ('cols', 'sub'))  31.2 us
    another operation x7, other arithmetic, orthonormal(): return jax.scipy.linalg.solve_triangular(lower, image, lower=True)  29.8 us
    psum x1, blocking collectives, on_device(): sums = lax.psum(jnp.sum(masked, axis=1), 'rows')  20.9 us
    psum x1, blocking collectives, on_device(): squares = lax.psum(jnp.sum(centered * centered, axis=1), 'rows')  15.8 us
    dot_general x3, matrix products, gram_of(): jnp.einsum('wkj,wlj->wkl', image, image, precision=lax.Precision.HIGHEST)  8.19 us
  transfers between devices with their start and end apart: 3, of which 3 were waited for; matrix products, arithmetic and copies ran while one was open for 0% of the time, Pallas kernels for 0%

commit v1 on v0

--- a/solution.py
+++ b/solution.py
@@ -5,6 +5,11 @@
 
 ASSETS = 8192
 ITERS = 3
+
+
+def one_after_other(array, first, second):
+    partial = lax.psum(array, first)
+    return lax.psum(partial, second)
 
 
 def gram_of(image):
@@ -42,7 +47,7 @@
     widened = scaled.astype(jnp.float32)
     factors = start_block
     for step in range(ITERS):
-        proj = lax.psum(project(factors, scaled), ("cols", "sub"))
+        proj = one_after_other(project(factors, scaled), "sub", "cols")
         image = lax.psum(expand(proj, widened), "rows")
         gram = lax.psum(gram_of(image), ("cols", "sub"))
         factors = orthonormal(image, gram)

time: 355 us -> 358 us (level)
    psum x3 -> x6, blocking collectives: 31.2 us -> 33.5 us  [the longest x3 23.2 us: one_after_other(): return lax.psum(partial, second)]
where the time goes in v1:
time: 358 us
  waiting for transfers between devices  153 us (43%)
  blocking collectives  106 us (30%)
  other arithmetic  67.2 us (19%)
  matrix products  17.9 us (5%)
  between operations  13.4 us (4%)
    psum x3, waiting for transfers between devices, on_device(): image = lax.psum(expand(proj, widened), 'rows')  153 us
    another operation x10, other arithmetic, orthonormal(): lower = jnp.linalg.cholesky(gram / ASSETS)  35.6 us
    psum x3, blocking collectives, on_device(): gram = lax.psum(gram_of(image), ('cols', 'sub'))  35.5 us
    another operation x7, other arithmetic, orthonormal(): return jax.scipy.linalg.solve_triangular(lower, image, lower=True)  29.8 us
    psum x3, blocking collectives, one_after_other(): return lax.psum(partial, second)  23.2 us
    psum x1, blocking collectives, on_device(): sums = lax.psum(jnp.sum(masked, axis=1), 'rows')  20.9 us
    psum x1, blocking collectives, on_device(): squares = lax.psum(jnp.sum(centered * centered, axis=1), 'rows')  15.8 us
    psum x3, blocking collectives, one_after_other(): partial = lax.psum(array, first)  10.2 us
  transfers between devices with their start and end apart: 3, of which 3 were waited for; matrix products, arithmetic and copies ran while one was open for 0% of the time, Pallas kernels for 0%

profile of v1, /device:TPU:0, one launch (start us, length us, event | category | flops | bytes accessed | tf_op | source)
XLA Modules:
  0.0 357.5 jit_solution(3543521484816449294)
XLA Ops:
  6.5 1.3 fusion
  7.9 20.9 %psum.98 = f32[4,2048]{1,0:T(4,128)S(1)} all-reduce(f32[4,2048]{1,0:T(4,128)S(1)} %fusion), channel_id=1, replica_groups=mesh['groups'=2,'rows'=4,'cols'=2,'sub'=2] {'rows'}, use_global_device_ids=true, to_apply=%region_1.0 | all-reduce | flops 8192 | bytes 65536 | tf_op jit(solution)/shard_map/psum | solution.py:42
  28.9 0.2 multiply_reduce_fusion
  29.1 15.8 %psum.99 = f32[4,2048]{1,0:T(4,128)S(1)} all-reduce(f32[4,2048]{1,0:T(4,128)S(1)} %multiply_reduce_fusion), channel_id=1, replica_groups=mesh['groups'=2,'rows'=4,'cols'=2,'sub'=2] {'rows'}, use_global_device_ids=true, to_apply=%region_3.0 | all-reduce | flops 8192 | bytes 65536 | tf_op jit(solution)/shard_map/psum | solution.py:45
  44.9 0.2 multiply_convert_fusion
  45.1 0.2 convolution_bitcast_fusion
  45.3 3.4 psum.100
  48.7 8.3 %psum.101 = f32[4,32,16]{1,2,0:T(8,128)S(1)} all-reduce(f32[4,32,16]{1,2,0:T(8,128)S(1)} %psum.100), channel_id=1, replica_groups=mesh['groups'=2,'rows'=4,'cols'=2,'sub'=2] {'cols'}, use_global_device_ids=true, to_apply=%region_5.0 | all-reduce | flops 2048 | bytes 16384 | tf_op jit(solution)/shard_map/psum | solution.py:12
  57.1 1.6 fusion.9
  58.7 0.0 all-reduce.4.cloned.1.call-update
  58.7 0.0 all-reduce.6.cloned.1.call-start
  58.8 50.5 %all-reduce.4.cloned.1.call-done = f32[4,32,2048]{2,1,0:T(8,128)} async-done(((f32[4,32,2048]{2,1,0:T(8,128)}), f32[4,32,2048]{2,1,0:T(8,128)}) %all-reduce.4.cloned.1.call-update) | async-done | bytes 1048592 | tf_op jit(solution)/shard_map/psum | solution.py:51
  109.3 2.7 fusion.10
  112.0 11.8 %psum.103 = f32[4,32,32]{1,2,0:T(8,128)S(1)} all-reduce(f32[4,32,32]{1,2,0:T(8,128)S(1)} %fusion.10), channel_id=1, replica_groups=mesh['groups'=2,'rows'=4,'cols'=2,'sub'=2] {'cols','sub'}, use_global_device_ids=true, to_apply=%region_7.0 | all-reduce | flops 4096 | bytes 32768 | tf_op jit(solution)/shard_map/psum | solution.py:52
  123.9 0.1 copy.12
  124.0 11.7 %custom-call.10 = f32[4,32,32]{2,1,0:T(8,128)S(1)} custom-call(f32[4,32,32]{2,1,0:T(8,128)S(1)} %fusion.8), custom_call_target="Cholesky" | custom-call | tf_op jit(solution)/shard_map/jit(cholesky)/cholesky | solution.py:29
  135.8 0.1 compare_reduce_fusion.2
  135.9 0.1 select_bitcast_fusion.2
  136.0 9.8 %custom-call.11 = f32[4,1,32,32]{2,3,1,0:T(8,128)S(1)} custom-call(f32[4,1,32,32]{3,2,1,0:T(8,128)S(1)} %select_bitcast_fusion.2), custom_call_target="InvertDiagBlocksLowerTriangular" | custom-call | tf_op jit(solution)/shard_map/jit(_solve_triangular)/vmap()/triangular_solve | solution.py:30
  145.8 1.1 convolution_convert_fusion.1
  146.9 0.2 fusion.11
  147.1 3.4 psum.104
  150.6 7.4 %psum.105 = f32[4,32,16]{1,2,0:T(8,128)S(1)} all-reduce(f32[4,32,16]{1,2,0:T(8,128)S(1)} %psum.104), channel_id=1, replica_groups=mesh['groups'=2,'rows'=4,'cols'=2,'sub'=2] {'cols'}, use_global_device_ids=true, to_apply=%region_11.0 | all-reduce | flops 2048 | bytes 16384 | tf_op jit(solution)/shard_map/psum | solution.py:12
  158.0 1.6 fusion.12
  159.6 0.0 all-reduce.6.cloned.1.call-update
  159.6 0.0 all-reduce.8.cloned.1.call-start
  159.7 51.2 %all-reduce.6.cloned.1.call-done = f32[4,32,2048]{2,1,0:T(8,128)} async-done(((f32[4,32,2048]{2,1,0:T(8,128)}), f32[4,32,2048]{2,1,0:T(8,128)}) %all-reduce.6.cloned.1.call-update) | async-done | bytes 1048592 | tf_op jit(solution)/shard_map/psum | solution.py:51
  210.9 2.7 fusion.13
  213.6 11.8 %psum.107 = f32[4,32,32]{1,2,0:T(8,128)S(1)} all-reduce(f32[4,32,32]{1,2,0:T(8,128)S(1)} %fusion.13), channel_id=1, replica_groups=mesh['groups'=2,'rows'=4,'cols'=2,'sub'=2] {'cols','sub'}, use_global_device_ids=true, to_apply=%region_13.0 | all-reduce | flops 4096 | bytes 32768 | tf_op jit(solution)/shard_map/psum | solution.py:52
  225.5 0.1 copy.14
  225.6 11.7 %custom-call.12 = f32[4,32,32]{2,1,0:T(8,128)S(1)} custom-call(f32[4,32,32]{2,1,0:T(8,128)S(1)} %fusion.6), custom_call_target="Cholesky" | custom-call | tf_op jit(solution)/shard_map/jit(cholesky)/cholesky | solution.py:29
  237.3 0.1 compare_reduce_fusion.1
  237.5 0.1 select_bitcast_fusion.1
  237.5 9.8 %custom-call.13 = f32[4,1,32,32]{2,3,1,0:T(8,128)S(1)} custom-call(f32[4,1,32,32]{3,2,1,0:T(8,128)S(1)} %select_bitcast_fusion.1), custom_call_target="InvertDiagBlocksLowerTriangular" | custom-call | tf_op jit(solution)/shard_map/jit(_solve_triangular)/vmap()/triangular_solve | solution.py:30
  247.4 1.1 convolution_convert_fusion
  248.5 0.2 fusion.14
  248.7 3.4 psum.108
  252.1 7.5 %psum.109 = f32[4,32,16]{1,2,0:T(8,128)S(1)} all-reduce(f32[4,32,16]{1,2,0:T(8,128)S(1)} %psum.108), channel_id=1, replica_groups=mesh['groups'=2,'rows'=4,'cols'=2,'sub'=2] {'cols'}, use_global_device_ids=true, to_apply=%region_15.0 | all-reduce | flops 2048 | bytes 16384 | tf_op jit(solution)/shard_map/psum | solution.py:12
  259.6 1.6 fusion.15
  261.2 51.2 %all-reduce.8.cloned.1.call-done = f32[4,32,2048]{2,1,0:T(8,128)} async-done(((f32[4,32,2048]{2,1,0:T(8,128)}), f32[4,32,2048]{2,1,0:T(8,128)}) %all-reduce.8.cloned.1.call-update) | async-done | bytes 1048592 | tf_op jit(solution)/shard_map/psum | solution.py:51
  312.5 2.7 fusion.16
  315.2 11.8 %psum.111 = f32[4,32,32]{1,2,0:T(8,128)S(1)} all-reduce(f32[4,32,32]{1,2,0:T(8,128)S(1)} %fusion.16), channel_id=1, replica_groups=mesh['groups'=2,'rows'=4,'cols'=2,'sub'=2] {'cols','sub'}, use_global_device_ids=true, to_apply=%region_17.20 | all-reduce | flops 4096 | bytes 32768 | tf_op jit(solution)/shard_map/psum | solution.py:52
  327.1 0.1 copy.16
  327.2 11.7 %custom-call.14 = f32[4,32,32]{2,1,0:T(8,128)S(1)} custom-call(f32[4,32,32]{2,1,0:T(8,128)S(1)} %fusion.4), custom_call_target="Cholesky" | custom-call | tf_op jit(solution)/shard_map/jit(cholesky)/cholesky | solution.py:29
  338.9 0.1 compare_reduce_fusion
  339.0 0.1 select_bitcast_fusion
  339.1 9.8 %custom-call.15 = f32[4,1,32,32]{2,3,1,0:T(8,128)S(1)} custom-call(f32[4,1,32,32]{3,2,1,0:T(8,128)S(1)} %select_bitcast_fusion), custom_call_target="InvertDiagBlocksLowerTriangular" | custom-call | tf_op jit(solution)/shard_map/jit(_solve_triangular)/vmap()/triangular_solve | solution.py:30
  349.0 2.0 fusion.2
  (28 shorter events, 0.3 us)
Async XLA Ops:
  6.5 22.3 %copy-start.3 = (f32[4,16,2048]{2,1,0:T(8,128)S(1)}, f32[4,16,2048]{2,1,0:T(8,128)}, u32[]{:S(2)}) copy-start(f32[4,16,2048]{2,1,0:T(8,128)} %param.6) | copy-start | bytes 1572868
  6.5 102.8 %all-reduce.4.cloned.1.call-start = ((), (), s32[]{:S(2)}) async-start(), calls=%async_computation | async-start | bytes 2097152 | tf_op jit(solution)/shard_map/psum | solution.py:51
  6.5 22.3 %copy-start.5 = (s32[4,2048]{1,0:T(4,128)S(1)}, s32[4,2048]{1,0:T(4,128)}, u32[]{:S(2)}) copy-start(s32[4,2048]{1,0:T(4,128)} %param.7) | copy-start | bytes 98308
  7.8 37.2 %copy-start.4 = (f32[4,32,2048]{2,1,0:T(8,128)S(1)}, f32[4,32,2048]{2,1,0:T(8,128)}, u32[]{:S(2)}) copy-start(f32[4,32,2048]{2,1,0:T(8,128)} %param.8) | copy-start | bytes 3145732
  58.7 152.2 %all-reduce.6.cloned.1.call-start = ((), (), s32[]{:S(2)}) async-start(), calls=%async_computation.1 | async-start | bytes 2097152 | tf_op jit(solution)/shard_map/psum | solution.py:51
  109.3 36.5 %copy-start = (f32[4,32,2048]{2,1,0:T(8,128)S(1)}, f32[4,32,2048]{2,1,0:T(8,128)}, u32[]{:S(2)}) copy-start(f32[4,32,2048]{2,1,0:T(8,128)} %all-reduce.4.cloned.1.call-done) | copy-start | bytes 3145732
  159.6 152.8 %all-reduce.8.cloned.1.call-start = ((), (), s32[]{:S(2)}) async-start(), calls=%async_computation.2 | async-start | bytes 2097152 | tf_op jit(solution)/shard_map/psum | solution.py:51
  210.9 36.5 %copy-start.1 = (f32[4,32,2048]{2,1,0:T(8,128)S(1)}, f32[4,32,2048]{2,1,0:T(8,128)}, u32[]{:S(2)}) copy-start(f32[4,32,2048]{2,1,0:T(8,128)} %all-reduce.6.cloned.1.call-done) | copy-start | bytes 3145732
  312.4 36.5 %copy-start.2 = (f32[4,32,2048]{2,1,0:T(8,128)S(1)}, f32[4,32,2048]{2,1,0:T(8,128)}, u32[]{:S(2)}) copy-start(f32[4,32,2048]{2,1,0:T(8,128)} %all-reduce.8.cloned.1.call-done) | copy-start | bytes 3145732
Sparse Core Ops, SparseCore 0:
  58.8 50.4 all-reduce.3
  159.7 51.0 all-reduce.5
  261.3 51.0 all-reduce.7
